TPU v7x, 32 devices: a whole 2x2x4 slice. The times are simulated.
32 devices in a mesh: pipe: 4 (over z), dp: 4 (over y, x), tensor: 2 (over core).
Axes of the slice: x: 2, y: 2, z: 4, core: 2. Of those that a mesh axis runs over, the one named last changes fastest.
Arguments:
- saved_inputs: bfloat16 [3, 2, 4, 512, 4096], P(None, None, 'pipe', 'dp', 'tensor'), may hold values from -6 to 6
- proj_in: bfloat16 [2, 4, 512, 4096], P(None, 'pipe', None, 'tensor'), may hold values from -0.09375 to 0.09375
- proj_out: bfloat16 [2, 4, 512, 4096], P(None, 'pipe', None, 'tensor'), may hold values from -0.25 to 0.25
- norm_gain: float32 [2, 4, 4096], P(None, 'pipe', 'tensor'), may hold values from 0.1 to 1.9
- arriving: bfloat16 [2, 4, 512, 4096], P(None, 'pipe', 'dp', 'tensor'), may hold values from -6 to 6
- logp_grad: bfloat16 [2, 512, 4096], P(None, 'dp', 'tensor'), may hold values from -6 to 6
- rewards: float32 [2, 4, 4], P(None, 'dp'), may hold values from -4 to 4
- seq_lengths: int32 [2, 4, 4], P(None, 'dp'), may hold values from 1 to 64, 128 in all within a row
- group_ids: int32 [2, 4, 4], P(None, 'dp'), may hold values from 0 to 3
Outputs:
- grad_in: float32 [2, 4, 512, 4096], P(None, 'pipe', 'dp', 'tensor')
- grad_out: float32 [2, 4, 512, 4096], P(None, 'pipe', 'dp', 'tensor')
- leaving: bfloat16 [2, 4, 512, 4096], P(None, 'pipe', 'dp', 'tensor')
Inputs may be any that keep to these rules, and one draw needn't show every extreme that they name: `seq_lengths`: the 4 lengths of one microbatch on one replica sum to 128. `group_ids`: groups take sequences from several replicas and microbatches.
All inputs are finite; a program needn't handle non-finite values.
Results may differ from a plain program's by a relative error of at most 0.023.
Values may be sent and summed in bfloat16 or wider, within the bound.
A program may use at most 128 MiB of HBM per device.

v0:
```python
import jax
import jax.numpy as jnp
from jax import lax
from jax.sharding import PartitionSpec as P

D = 4096
EPS = 1e-05


def shifted(x, axis, by):
    count = lax.axis_size(axis)
    return lax.ppermute(x, axis, [(i, (i + by) % count) for i in range(count)])


def silu_slope(values):
    sigma = jax.nn.sigmoid(values)
    return sigma * (1.0 + values * (1.0 - sigma))


def block_back(inputs, arrive, weight_in, weight_out, gain_rows, inv_rms):
    inputs_f = inputs.astype(jnp.float32)
    gained = (inputs_f * gain_rows[:, None, :]).astype(jnp.bfloat16)
    part_pre = jnp.einsum("vrd,vkd->vrk", gained, weight_in, preferred_element_type=jnp.float32)
    part_back = jnp.einsum("vrd,vkd->vrk", arrive, weight_out, preferred_element_type=jnp.float32)
    pre_sum, back_sum = (
        lax.psum(part_pre.astype(jnp.bfloat16), "tensor").astype(jnp.float32),
        lax.psum(part_back.astype(jnp.bfloat16), "tensor").astype(jnp.float32),
    )
    scaled = inv_rms[..., None]
    pre_act = scaled * pre_sum
    hidden = jax.nn.silu(pre_act).astype(jnp.bfloat16)
    grad_pre = back_sum * silu_slope(pre_act)
    grad_scaled = (scaled * grad_pre).astype(jnp.bfloat16)
    term_in = jnp.einsum("vrk,vrd->vkd", grad_scaled, gained, preferred_element_type=jnp.float32)
    term_out = jnp.einsum("vrk,vrd->vkd", hidden, arrive, preferred_element_type=jnp.float32)
    grad_gained = jnp.einsum(
        "vrk,vkd->vrd", grad_scaled, weight_in, preferred_element_type=jnp.float32
    )
    radial_sum = jnp.sum(grad_pre * pre_sum, axis=-1)
    out_cot = (
        arrive.astype(jnp.float32)
        + gain_rows[:, None, :] * grad_gained
        - inputs_f * (inv_rms**3 * radial_sum / D)[..., None]
    )
    return (out_cot.astype(jnp.bfloat16), term_in, term_out)


def shards(
    saved_inputs, proj_in, proj_out, norm_gain, arriving, logp_grad, rewards, seq_lengths, group_ids
):
    sections = lax.axis_size("pipe")
    section = lax.axis_index("pipe")
    replicas = lax.axis_size("dp")
    saved = saved_inputs[:, :, 0]
    weights_in = proj_in[:, 0]
    weights_out = proj_out[:, 0]
    gains = norm_gain[:, 0]
    current = arriving[:, 0]
    step_count = saved.shape[0]
    local_rows = saved.shape[2]
    new_count = logp_grad.shape[0]
    seq_count = rewards.shape[2]
    group_count = new_count * replicas * seq_count // 8
    saved_f = saved.astype(jnp.float32)
    squares = jnp.sum(saved_f * saved_f, axis=-1)
    totals = lax.psum(squares, "tensor")
    inv_rms_all = 1.0 / jnp.sqrt(totals / D + EPS)
    groups = jnp.arange(group_count, dtype=jnp.int32)
    member = (group_ids[..., None] == groups).astype(jnp.float32)
    sums = jnp.sum(member * rewards[..., None], axis=(0, 1, 2))
    counts = jnp.sum(member, axis=(0, 1, 2))
    sums, counts = lax.psum((sums, counts), "dp")
    means = sums / jnp.maximum(counts, 1.0)
    advantage = rewards - jnp.sum(member * means, axis=-1)
    ends = jnp.cumsum(seq_lengths, axis=-1)
    position = jnp.arange(local_rows, dtype=jnp.int32)
    segment = jnp.sum((position[:, None] >= ends[..., None, :]).astype(jnp.int32), axis=-1)
    pick = (segment[..., None] == jnp.arange(seq_count, dtype=jnp.int32)).astype(jnp.float32)
    token_weight = jnp.sum(pick * advantage[..., None, :], axis=-1)[:, 0]
    entering = (-token_weight[..., None] * logp_grad.astype(jnp.float32)).astype(jnp.bfloat16)

    def run_blocks(first, last, arrive, step_index):
        return block_back(
            saved[step_index, first:last],
            arrive,
            weights_in,
            weights_out,
            gains,
            inv_rms_all[step_index, first:last],
        )

    is_top = section == sections - 1
    acc_in = jnp.zeros((2,) + weights_in.shape[1:], jnp.float32)
    acc_out = jnp.zeros((2,) + weights_in.shape[1:], jnp.float32)
    for step_index in range(step_count - 1):
        moved, add_in, add_out = run_blocks(0, 2, current, step_index)
        acc_in = acc_in + add_in
        acc_out = acc_out + add_out
        received = shifted(moved, "pipe", -1)
        from_upper = received[1]
        from_lower = received[0]
        upper_next = jnp.where(is_top, entering[step_index], from_upper)
        lower_next = jnp.where(is_top, from_upper, from_lower)
        current = jnp.stack([lower_next, upper_next])
    final_index = step_count - 1
    leaving, add_in, add_out = run_blocks(0, 2, current, final_index)
    summed_in, summed_out = (
        lax.psum_scatter(
            (acc_in + add_in).astype(jnp.bfloat16), "dp", scatter_dimension=1, tiled=True
        ).astype(jnp.float32),
        lax.psum_scatter(
            (acc_out + add_out).astype(jnp.bfloat16), "dp", scatter_dimension=1, tiled=True
        ).astype(jnp.float32),
    )
    scale = 1.0 / (replicas * local_rows)
    return ((summed_in * scale)[:, None], (summed_out * scale)[:, None], leaving[:, None])


def solution(mesh):
    return jax.shard_map(
        shards,
        mesh=mesh,
        in_specs=(
            P(None, None, "pipe", "dp", "tensor"),
            P(None, "pipe", None, "tensor"),
            P(None, "pipe", None, "tensor"),
            P(None, "pipe", "tensor"),
            P(None, "pipe", "dp", "tensor"),
            P(None, "dp", "tensor"),
            P(None, "dp", None),
            P(None, "dp", None),
            P(None, "dp", None),
        ),
        out_specs=(
            P(None, "pipe", "dp", "tensor"),
            P(None, "pipe", "dp", "tensor"),
            P(None, "pipe", "dp", "tensor"),
        ),
        check_vma=False,
    )
```

profile of v0, /device:TPU:0, one launch (start us, length us, event | category | flops | bytes accessed | tf_op | source)
XLA Modules:
  0.0 281.6 jit_solution(14688957267595545626)
XLA Ops:
  7.2 0.9 copy.46
  8.1 4.8 %fusion.43 = bf16[2,128,512]{2,1,0:T(8,128)(2,1)} fusion(bf16[2,1,512,2048]{3,2,1,0:T(8,128)(2,1)} %param.11, bf16[2,1,128,2048]{3,2,1,0:T(8,128)(2,1)} %param.13), kind=kOutput, calls=%fused_computation.43 | convolution fusion | flops 537001984 | bytes 5505024 | tf_op jit(solution)/shard_map/vrd,vkd->vrk/dot_general | solution.py:24
  12.9 4.4 %fusion.52 = bf16[2,128,512]{2,1,0:T(8,128)(2,1)} fusion(bf16[2,1,512,2048]{3,2,1,0:T(8,128)(2,1)} %param.10, f32[2,2048]{1,0:T(2,128)S(1)} %bitcast.130, bf16[3,2,1,128,2048]{4,3,1,2,0:T(8,128)(2,1)S(1)} %bitcast.121), kind=kOutput, calls=%fused_computation.46 | convolution fusion | flops 538574848 | bytes 5521408 | tf_op jit(solution)/shard_map/vrd,vkd->vrk/dot_general | solution.py:23
  17.3 0.0 all-reduce.10.cloned.1.call-start
  17.4 0.7 multiply_reduce_fusion
  18.1 0.1 convert_reduce_fusion
  18.2 11.4 %all-reduce = (f32[4]{0:T(128)S(1)}, f32[4]{0:T(128)S(1)}) all-reduce(f32[4]{0:T(128)S(1)} %get-tuple-element.10, f32[4]{0:T(128)S(1)} %get-tuple-element.9), channel_id=1, replica_groups=mesh['pipe'=4,'dp'=4,'tensor'=2] {'dp'}, use_global_device_ids=true, to_apply=%region_8.9 | all-reduce | flops 8 | bytes 64 | tf_op jit(solution)/shard_map/psum | solution.py:72
  29.5 0.2 select_reduce_fusion.1
  29.7 0.2 reduce_window_sum.14
  29.9 2.4 psum.63
  32.4 6.5 %all-reduce.12.cloned.1.call-done = (bf16[2,128,512]{2,1,0:T(8,128)(2,1)}, bf16[2,128,512]{2,1,0:T(8,128)(2,1)}) async-done(((bf16[2,128,512]{2,1,0:T(8,128)(2,1)}, bf16[2,128,512]{2,1,0:T(8,128)(2,1)}), (bf16[2,128,512]{2,1,0:T(8,128)(2,1)}, bf16[2,128,512]{2,1,0:T(8,128)(2,1)})) %all-reduce.12.cloned.1.call-update) | async-done | bytes 524304 | tf_op jit(solution)/shard_map/psum | solution.py:26
  38.9 1.4 fusion.93
  40.3 5.0 %fusion.33 = bf16[2,128,2048]{2,1,0:T(8,128)(2,1)} fusion(bf16[2,1,512,2048]{3,2,1,0:T(8,128)(2,1)} %param.10, bf16[2,1,128,2048]{3,2,1,0:T(8,128)(2,1)} %param.13, f32[2,128]{1,0:T(2,128)S(1)} %fusion.121, f32[2,2048]{1,0:T(2,128)S(1)} %bitcast.131, bf16[3,2,1,128,2048]{4,3,1,2,0:T(8,128)(2,1)S(1)} %bitcast.122, f32[2,128]{1,0:T(2,128)S(1)} %get-tuple-element.25, ...), kind=kOutput, calls=%fused_computation.32 | convolution fusion | flops 542244864 | bytes 7882752 | tf_op jit(solution)/shard_map/vrk,vkd->vrd/dot_general | solution.py:36
  45.3 3.6 %collective-permute-start = (bf16[2,128,2048]{2,1,0:T(8,128)(2,1)}, bf16[2,128,2048]{2,1,0:T(8,128)(2,1)}, u32[]{:S(2)}, u32[]{:S(2)}) collective-permute-start(bf16[2,128,2048]{2,1,0:T(8,128)(2,1)} %fusion.33), channel_id=1, source_target_pairs={{0,24},{8,0},{16,8},{24,16},{1,25},{9,1},{17,9},{25,17},{2,26},{10... | collective-permute-start | bytes 3145736 | tf_op jit(solution)/shard_map/ppermute | solution.py:12
  48.9 0.1 convert_reduce_fusion.1
  49.0 0.1 select_reduce_fusion
  49.1 4.5 %fusion.55 = bf16[2,128,512]{2,1,0:T(8,128)(2,1)} fusion(bf16[2,1,512,2048]{3,2,1,0:T(8,128)(2,1)} %param.10, f32[2,2048]{1,0:T(2,128)S(1)} %bitcast.132, bf16[3,2,1,128,2048]{4,3,1,2,0:T(8,128)(2,1)S(1)} %bitcast.123), kind=kOutput, calls=%fused_computation.47 | convolution fusion | flops 538574848 | bytes 5521408 | tf_op jit(solution)/shard_map/vrd,vkd->vrk/dot_general | solution.py:23
  53.6 0.2 multiply_convert_fusion
  53.9 18.2 %collective-permute-done = bf16[2,128,2048]{2,1,0:T(8,128)(2,1)} collective-permute-done((bf16[2,128,2048]{2,1,0:T(8,128)(2,1)}, bf16[2,128,2048]{2,1,0:T(8,128)(2,1)}, u32[]{:S(2)}, u32[]{:S(2)}) %collective-permute-start) | collective-permute-done | bytes 1048608 | tf_op jit(solution)/shard_map/ppermute | solution.py:12
  72.1 1.3 slice_select_fusion.3
  73.4 0.8 copy-done.11
  74.2 0.2 copy-done.13
  74.3 2.2 fusion.46
  76.6 20.6 %all-reduce.10.cloned.1.call-done = (bf16[2,128,512]{2,1,0:T(8,128)(2,1)}, bf16[2,128,512]{2,1,0:T(8,128)(2,1)}) async-done(((bf16[2,128,512]{2,1,0:T(8,128)(2,1)}, bf16[2,128,512]{2,1,0:T(8,128)(2,1)}), (bf16[2,128,512]{2,1,0:T(8,128)(2,1)}, bf16[2,128,512]{2,1,0:T(8,128)(2,1)})) %all-reduce.10.cloned.1.call-update) | async-done | bytes 524304 | tf_op jit(solution)/shard_map/psum | solution.py:26
  97.2 1.4 fusion.101
  98.7 4.1 %fusion.39 = bf16[2,128,2048]{2,1,0:T(8,128)(2,1)S(1)} fusion(f32[2,128]{1,0:T(2,128)S(1)} %fusion.123, bf16[2,1,512,2048]{3,2,1,0:T(8,128)(2,1)} %param.10, f32[2,2048]{1,0:T(2,128)S(1)} %bitcast.133, bf16[3,2,1,128,2048]{4,3,1,2,0:T(8,128)(2,1)S(1)} %bitcast.124, bf16[1,128,2048]{2,1,0:T(8,128)(2,1)} %copy-done.13, bf16[1,128,2048]{2,1,0:T(8,128)(2,1)} %copy-done.11, ...), kind=kOutput, calls=%fused_computation.36 | convolution fusion | flops 542769152 | bytes 7882752 | tf_op jit(solution)/shard_map/vrk,vkd->vrd/dot_general | solution.py:36
  102.8 3.7 %collective-permute-start.1 = (bf16[2,128,2048]{2,1,0:T(8,128)(2,1)S(1)}, bf16[2,128,2048]{2,1,0:T(8,128)(2,1)S(1)}, u32[]{:S(2)}, u32[]{:S(2)}) collective-permute-start(bf16[2,128,2048]{2,1,0:T(8,128)(2,1)S(1)} %fusion.39), channel_id=1, source_target_pairs={{0,24},{8,0},{16,8},{24,16},{1,25},{9,1},{17,9},{25,17},{2,26},{10... | collective-permute-start | bytes 3145736 | tf_op jit(solution)/shard_map/ppermute | solution.py:12
  106.5 2.2 fusion.58
  108.7 20.6 %collective-permute-done.1 = bf16[2,128,2048]{2,1,0:T(8,128)(2,1)S(1)} collective-permute-done((bf16[2,128,2048]{2,1,0:T(8,128)(2,1)S(1)}, bf16[2,128,2048]{2,1,0:T(8,128)(2,1)S(1)}, u32[]{:S(2)}, u32[]{:S(2)}) %collective-permute-start.1) | collective-permute-done | bytes 1048608 | tf_op jit(solution)/shard_map/ppermute | solution.py:12
  129.4 0.1 slice_select_fusion.1
  129.5 0.8 copy-done.9
  130.2 0.2 copy-done.10
  130.4 2.2 fusion.49
  132.6 0.2 reduce-scatter.5.cloned.1.call-start
  132.9 5.9 %fusion.62 = f32[2,512,2048]{2,1,0:T(8,128)} fusion(bf16[2,1,128,2048]{3,2,1,0:T(8,128)(2,1)} %param.13, bf16[2,128,512]{2,1,0:T(8,128)(2,1)S(1)} %copy-done.6, f32[2,128]{1,0:T(2,128)S(1)} %get-tuple-element.25), kind=kOutput, calls=%fused_computation.55 | convolution fusion | flops 537788416 | bytes 9700352 | tf_op jit(solution)/shard_map/vrk,vrd->vkd/dot_general | solution.py:35
  138.9 4.6 %fusion.110 = f32[2,512,2048]{2,1,0:T(8,128)} fusion(bf16[1,128,2048]{2,1,0:T(8,128)(2,1)S(1)} %copy-done.14, bf16[1,128,2048]{2,1,0:T(8,128)(2,1)S(1)} %copy-done.12, bf16[2,128,512]{2,1,0:T(8,128)(2,1)S(1)} %copy-done.7, f32[2,128]{1,0:T(2,128)S(1)} %get-tuple-element.24), kind=kOutput, calls=%fused_computation.106 | convolution fusion | flops 538312704 | bytes 9700352 | tf_op jit(solution)/shard_map/vrk,vrd->vkd/dot_general | solution.py:35
  143.4 9.9 %all-reduce.8.cloned.1.call-done = (bf16[2,128,512]{2,1,0:T(8,128)(2,1)}, bf16[2,128,512]{2,1,0:T(8,128)(2,1)}) async-done(((bf16[2,128,512]{2,1,0:T(8,128)(2,1)}, bf16[2,128,512]{2,1,0:T(8,128)(2,1)}), (bf16[2,128,512]{2,1,0:T(8,128)(2,1)}, bf16[2,128,512]{2,1,0:T(8,128)(2,1)})) %all-reduce.8.cloned.1.call-update) | async-done | bytes 524304 | tf_op jit(solution)/shard_map/psum | solution.py:26
  153.3 9.5 %add_convert_fusion = bf16[2,512,2048]{2,1,0:T(8,128)(2,1)} fusion(f32[2,512,2048]{2,1,0:T(8,128)} %fusion.62, f32[2,512,2048]{2,1,0:T(8,128)} %fusion.110, bf16[1,128,2048]{2,1,0:T(8,128)(2,1)} %copy-done.10, bf16[1,128,2048]{2,1,0:T(8,128)(2,1)} %copy-done.9, bf16[2,128,512]{2,1,0:T(8,128)(2,1)} %get-tuple-element.13, f32[2,128]{1,0:T(2,128)S(1)} %get-tuple-element.23), kind=kOutput, calls=%fused_computation | convolution fusion | flops 544604160 | bytes 22283264 | tf_op jit(solution)/shard_map/vrk,vrd->vkd/dot_general | solution.py:35
  162.9 0.0 reduce-scatter.3.cloned.1.call-start
  162.9 2.4 fusion.74
  165.4 1.4 fusion.71
  166.9 3.7 %add_convert_fusion.1 = bf16[2,512,2048]{2,1,0:T(8,128)(2,1)} fusion(f32[2,512,2048]{2,1,0:T(8,128)S(1)} %fusion.74, f32[2,512,2048]{2,1,0:T(8,128)S(1)} %fusion.71, f32[2,2048]{1,0:T(2,128)S(1)} %bitcast.137, bf16[3,2,1,128,2048]{4,3,1,2,0:T(8,128)(2,1)S(1)} %bitcast.128, f32[2,128]{1,0:T(2,128)S(1)} %get-tuple-element.23, ...), kind=kOutput, calls=%fused_computation.1 | convolution fusion | flops 546439168 | bytes 22561792 | tf_op jit(solution)/shard_map/vrk,vrd->vkd/dot_general | solution.py:34
  170.5 1.4 fusion.109
  172.0 4.8 %fusion.61 = bf16[2,1,128,2048]{3,2,1,0:T(8,128)(2,1)} fusion(f32[2,128]{1,0:T(2,128)S(1)} %fusion.125, bf16[2,1,512,2048]{3,2,1,0:T(8,128)(2,1)} %param.10, f32[2,2048]{1,0:T(2,128)S(1)} %bitcast.138, bf16[3,2,1,128,2048]{4,3,1,2,0:T(8,128)(2,1)S(1)} %bitcast.129, bf16[1,128,2048]{2,1,0:T(8,128)(2,1)} %copy-done.10, bf16[1,128,2048]{2,1,0:T(8,128)(2,1)} %copy-done.9, ...), kind=kOutput, calls=%fused_computation.49 | convolution fusion | flops 542769152 | bytes 7882752 | tf_op jit(solution)/shard_map/vrk,vkd->vrd/dot_general | solution.py:36
  176.9 40.0 %reduce-scatter.5.cloned.1.call-done = bf16[2,128,2048]{2,1,0:T(8,128)(2,1)} async-done(((bf16[2,512,2048]{2,1,0:T(8,128)(2,1)}), bf16[2,128,2048]{2,1,0:T(8,128)(2,1)}) %reduce-scatter.5.cloned.1.call-update) | async-done | bytes 1048592 | tf_op jit(solution)/shard_map/reduce_scatter | solution.py:111
  216.8 2.8 multiply_bitcast_fusion
  219.6 52.7 %reduce-scatter.3.cloned.1.call-done = bf16[2,128,2048]{2,1,0:T(8,128)(2,1)} async-done(((bf16[2,512,2048]{2,1,0:T(8,128)(2,1)}), bf16[2,128,2048]{2,1,0:T(8,128)(2,1)}) %reduce-scatter.3.cloned.1.call-update) | async-done | bytes 1048592 | tf_op jit(solution)/shard_map/reduce_scatter | solution.py:108
  272.3 2.8 multiply_bitcast_fusion.1
  (55 shorter events, 0.3 us)
Async XLA Ops:
  7.2 5.7 %copy-start = (bf16[3,2,1,128,2048]{4,3,2,1,0:T(8,128)(2,1)S(1)}, bf16[3,2,1,128,2048]{4,3,2,1,0:T(8,128)(2,1)}, u32[]{:S(2)}) copy-start(bf16[3,2,1,128,2048]{4,3,2,1,0:T(8,128)(2,1)} %param.9) | copy-start | bytes 9437188
  7.2 31.7 %all-reduce.12.cloned.1.call-start = ((), (), s32[]{:S(2)}) async-start(), calls=%async_computation.6 | async-start | bytes 1048576 | tf_op jit(solution)/shard_map/psum | solution.py:26
  17.3 0.8 copy-start.18
  17.3 0.8 copy-start.19
  17.3 12.4 %copy-start.20 = (s32[2,1,4]{2,1,0:T(1,128)S(1)}, s32[2,1,4]{2,1,0:T(1,128)}, u32[]{:S(2)}) copy-start(s32[2,1,4]{2,1,0:T(1,128)} %param.16) | copy-start | bytes 100
  17.3 79.9 %all-reduce.10.cloned.1.call-start = ((), (), s32[]{:S(2)}) async-start(), calls=%async_computation.5 | async-start | bytes 1048576 | tf_op jit(solution)/shard_map/psum | solution.py:26
  45.3 26.8 %collective-permute-start = (bf16[2,128,2048]{2,1,0:T(8,128)(2,1)}, bf16[2,128,2048]{2,1,0:T(8,128)(2,1)}, u32[]{:S(2)}, u32[]{:S(2)}) collective-permute-start(bf16[2,128,2048]{2,1,0:T(8,128)(2,1)} %fusion.33), channel_id=1, source_target_pairs={{0,24},{8,0},{16,8},{24,16},{1,25},{9,1},{17,9},{25,17},{2,26},{10... | collective-permute-start | bytes 3145736 | tf_op jit(solution)/shard_map/ppermute | solution.py:12
  49.1 4.5 %copy-start.17 = (bf16[2,128,2048]{2,1,0:T(8,128)(2,1)S(1)}, bf16[2,128,2048]{2,1,0:T(8,128)(2,1)}, u32[]{:S(2)}) copy-start(bf16[2,128,2048]{2,1,0:T(8,128)(2,1)} %param.14) | copy-start | bytes 3145732
  53.6 20.7 %copy-start.1 = (bf16[2,1,512,2048]{3,2,1,0:T(8,128)(2,1)S(1)}, bf16[2,1,512,2048]{3,2,1,0:T(8,128)(2,1)}, u32[]{:S(2)}) copy-start(bf16[2,1,512,2048]{3,2,1,0:T(8,128)(2,1)} %param.11) | copy-start | bytes 12582916
  53.9 18.2 %copy-start.3 = (bf16[2,128,2048]{2,1,0:T(8,128)(2,1)}, bf16[2,128,2048]{2,1,0:T(8,128)(2,1)S(1)}, u32[]{:S(2)}) copy-start(bf16[2,128,2048]{2,1,0:T(8,128)(2,1)S(1)} %multiply_convert_fusion) | copy-start | bytes 3145732
  73.4 0.8 copy-start.11
  73.4 1.0 copy-start.13
  76.6 76.8 %all-reduce.8.cloned.1.call-start = ((), (), s32[]{:S(2)}) async-start(), calls=%async_computation.4 | async-start | bytes 1048576 | tf_op jit(solution)/shard_map/psum | solution.py:26
  98.7 7.8 %copy-start.21 = (bf16[2,1,512,2048]{3,2,1,0:T(8,128)(2,1)S(1)}, bf16[2,1,512,2048]{3,2,1,0:T(8,128)(2,1)}, u32[]{:S(2)}) copy-start(bf16[2,1,512,2048]{3,2,1,0:T(8,128)(2,1)} %param.10) | copy-start | bytes 12582916
  102.8 26.6 %copy-start.4 = (bf16[2,128,2048]{2,1,0:T(8,128)(2,1)S(1)}, bf16[2,128,2048]{2,1,0:T(8,128)(2,1)}, u32[]{:S(2)}) copy-start(bf16[2,128,2048]{2,1,0:T(8,128)(2,1)} %copy-done.3) | copy-start | bytes 3145732
  102.8 27.6 %copy-start.2 = (bf16[2,1,512,2048]{3,2,1,0:T(8,128)(2,1)S(1)}, bf16[2,1,512,2048]{3,2,1,0:T(8,128)(2,1)}, u32[]{:S(2)}) copy-start(bf16[2,1,512,2048]{3,2,1,0:T(8,128)(2,1)} %param.11) | copy-start | bytes 12582916
  102.8 26.5 %collective-permute-start.1 = (bf16[2,128,2048]{2,1,0:T(8,128)(2,1)S(1)}, bf16[2,128,2048]{2,1,0:T(8,128)(2,1)S(1)}, u32[]{:S(2)}, u32[]{:S(2)}) collective-permute-start(bf16[2,128,2048]{2,1,0:T(8,128)(2,1)S(1)} %fusion.39), channel_id=1, source_target_pairs={{0,24},{8,0},{16,8},{24,16},{1,25},{9,1},{17,9},{25,17},{2,26},{10... | collective-permute-start | bytes 3145736 | tf_op jit(solution)/shard_map/ppermute | solution.py:12
  129.4 0.8 copy-start.9
  129.5 1.0 copy-start.10
  129.5 3.4 %copy-start.6 = (bf16[2,128,512]{2,1,0:T(8,128)(2,1)S(1)}, bf16[2,128,512]{2,1,0:T(8,128)(2,1)}, u32[]{:S(2)}) copy-start(bf16[2,128,512]{2,1,0:T(8,128)(2,1)} %get-tuple-element.17) | copy-start | bytes 786436
  132.6 84.2 %reduce-scatter.5.cloned.1.call-start = ((), (), s32[]{:S(2)}) async-start(), calls=%async_computation.3 | async-start | bytes 5242880 | tf_op jit(solution)/shard_map/reduce_scatter | solution.py:111
  132.9 6.0 %copy-start.7 = (bf16[2,128,512]{2,1,0:T(8,128)(2,1)S(1)}, bf16[2,128,512]{2,1,0:T(8,128)(2,1)}, u32[]{:S(2)}) copy-start(bf16[2,128,512]{2,1,0:T(8,128)(2,1)} %get-tuple-element.15) | copy-start | bytes 786436
  132.9 6.0 %copy-start.12 = (bf16[1,128,2048]{2,1,0:T(8,128)(2,1)S(1)}, bf16[1,128,2048]{2,1,0:T(8,128)(2,1)}, u32[]{:S(2)}) copy-start(bf16[1,128,2048]{2,1,0:T(8,128)(2,1)} %copy-done.11) | copy-start | bytes 1572868
  132.9 5.9 %copy-start.14 = (bf16[1,128,2048]{2,1,0:T(8,128)(2,1)S(1)}, bf16[1,128,2048]{2,1,0:T(8,128)(2,1)}, u32[]{:S(2)}) copy-start(bf16[1,128,2048]{2,1,0:T(8,128)(2,1)} %copy-done.13) | copy-start | bytes 1572868
  162.9 109.4 %reduce-scatter.3.cloned.1.call-start = ((), (), s32[]{:S(2)}) async-start(), calls=%async_computation.2 | async-start | bytes 5242880 | tf_op jit(solution)/shard_map/reduce_scatter | solution.py:108
  162.9 2.5 copy-start.8
  162.9 2.5 copy-start.16
  165.4 1.5 copy-start.5
  165.4 1.5 copy-start.15
Sparse Core Ops, SparseCore 0:
  17.4 21.3 all-reduce.11
  76.7 20.5 all-reduce.9
  132.8 20.5 all-reduce.7
  163.0 53.7 reduce-scatter.4
  219.6 52.6 reduce-scatter.2
where the time goes:
time: 282 us
  waiting for transfers between devices  169 us (60%)
  matrix products  61.7 us (22%)
  between operations  14.1 us (5%)
  blocking collectives  13.8 us (5%)
  other arithmetic  12.9 us (5%)
  starting transfers between devices  7.7 us (3%)
  local copies, waits for them, and re-layouts  2.86 us (1%)
    reduce_scatter x1, waiting for transfers between devices, shards(): lax.psum_scatter((acc_in + add_in).astype(jnp.bfloat16), 'dp', scatter_di...  52.7 us
    reduce_scatter x1, waiting for transfers between devices, shards(): lax.psum_scatter((acc_out + add_out).astype(jnp.bfloat16), 'dp', scatter_...  40 us
    ppermute x2, waiting for transfers between devices, shifted(): return lax.ppermute(x, axis, [(i, (i + by) % count) for i in range(count)])  38.8 us
    psum x3, waiting for transfers between devices, block_back(): lax.psum(part_pre.astype(jnp.bfloat16), 'tensor').astype(jnp.float32)  37 us
    dot_general x3, matrix products, block_back(): jnp.einsum('vrk,vrd->vkd', hidden, arrive, preferred_element_type=jnp.flo...  20 us
    dot_general x3, matrix products, block_back(): jnp.einsum('vrk,vkd->vrd', grad_scaled, weight_in, preferred_element_type...  13.9 us
    psum x1, blocking collectives, shards(): sums, counts = lax.psum((sums, counts), 'dp')  11.4 us
    dot_general x3, matrix products, block_back(): jnp.einsum('vrd,vkd->vrk', gained, weight_in, preferred_element_type=jnp....  11.1 us
  transfers between devices with their start and end apart: 7, of which 7 were waited for; matrix products, arithmetic and copies ran while one was open for 13% of the time, Pallas kernels for 0%

commit v1 on v0

--- a/solution.py
+++ b/solution.py
@@ -5,6 +5,11 @@
 
 D = 4096
 EPS = 1e-05
+
+
+def gather_and_add(value, axis):
+    parts = lax.all_gather(value, axis)
+    return jnp.sum(parts, axis=0)
 
 
 def shifted(x, axis, by):
@@ -23,7 +28,7 @@
     part_pre = jnp.einsum("vrd,vkd->vrk", gained, weight_in, preferred_element_type=jnp.float32)
     part_back = jnp.einsum("vrd,vkd->vrk", arrive, weight_out, preferred_element_type=jnp.float32)
     pre_sum, back_sum = (
-        lax.psum(part_pre.astype(jnp.bfloat16), "tensor").astype(jnp.float32),
+        gather_and_add(part_pre.astype(jnp.bfloat16), "tensor").astype(jnp.float32),
         lax.psum(part_back.astype(jnp.bfloat16), "tensor").astype(jnp.float32),
     )
     scaled = inv_rms[..., None]

time: 282 us -> 271 us (0.961)
  waiting for transfers between devices: 169 us -> 134 us
  matrix products: 61.7 us -> 72.8 us
  blocking collectives: 13.8 us -> 21 us
  other arithmetic: 12.9 us -> 18.7 us
    psum x3, waiting for transfers between devices: 37 us -> 12.3 us  [block_back(): lax.psum(part_back.astype(jnp.bfloat16), 'tensor').astype(jnp.float32)]
    dot_general x3, matrix products: 7.51 us -> 19.7 us  [block_back(): jnp.einsum('vrk,vrd->vkd', grad_scaled, gained, preferred_element_type=jn...]
    ppermute x2, waiting for transfers between devices: 38.8 us -> 28.4 us  [shifted(): return lax.ppermute(x, axis, [(i, (i + by) % count) for i in range(count)])]
    all_gather x0 -> x3, blocking collectives: none -> 7.12 us  [gather_and_add(): parts = lax.all_gather(value, axis)]
    reduce_sum x0 -> x3, other arithmetic: none -> 3.47 us  [gather_and_add(): return jnp.sum(parts, axis=0)]
  transfers between devices with their start and end apart: 7 -> 7, of which waited for: 7 -> 6; matrix products, arithmetic and copies ran while one was open for 13% -> 24% of each run, Pallas kernels for 0% -> 0%
where the time goes in v1:
time: 271 us; the launch traced here: 270 us
  waiting for transfers between devices  134 us (49%)
  matrix products  72.8 us (27%)
  blocking collectives  21 us (8%)
  other arithmetic  18.7 us (7%)
  between operations  14.1 us (5%)
  starting transfers between devices  7.45 us (3%)
    reduce_scatter x1, waiting for transfers between devices, shards(): lax.psum_scatter((acc_in + add_in).astype(jnp.bfloat16), 'dp', scatter_di...  52.7 us
    reduce_scatter x1, waiting for transfers between devices, shards(): lax.psum_scatter((acc_out + add_out).astype(jnp.bfloat16), 'dp', scatter_...  41 us
    ppermute x2, waiting for transfers between devices, shifted(): return lax.ppermute(x, axis, [(i, (i + by) % count) for i in range(count)])  28.4 us
    dot_general x3, matrix products, block_back(): jnp.einsum('vrk,vrd->vkd', hidden, arrive, preferred_element_type=jnp.flo...  20.1 us
    dot_general x3, matrix products, block_back(): jnp.einsum('vrk,vrd->vkd', grad_scaled, gained, preferred_element_type=jn...  19.7 us
    dot_general x3, matrix products, block_back(): jnp.einsum('vrk,vkd->vrd', grad_scaled, weight_in, preferred_element_type...  14.7 us
    psum x3, waiting for transfers between devices, block_back(): lax.psum(part_back.astype(jnp.bfloat16), 'tensor').astype(jnp.float32)  12.3 us
    psum x1, blocking collectives, shards(): sums, counts = lax.psum((sums, counts), 'dp')  11.2 us
  transfers between devices with their start and end apart: 7, of which 6 were waited for; matrix products, arithmetic and copies ran while one was open for 24% of the time, Pallas kernels for 0%

profile of v1, /device:TPU:0, one launch (start us, length us, event | category | flops | bytes accessed | tf_op | source)
XLA Modules:
  0.0 270.4 jit_solution(16351129438634758896)
XLA Ops:
  7.3 4.9 %fusion.43 = bf16[2,128,512]{2,1,0:T(8,128)(2,1)} fusion(bf16[2,1,512,2048]{3,2,1,0:T(8,128)(2,1)} %param.11, bf16[2,1,128,2048]{3,2,1,0:T(8,128)(2,1)} %param.13), kind=kOutput, calls=%fused_computation.43 | convolution fusion | flops 537001984 | bytes 5505024 | tf_op jit(solution)/shard_map/vrd,vkd->vrk/dot_general | solution.py:29
  12.3 0.7 multiply_reduce_fusion
  12.9 2.6 psum.42
  15.6 0.1 convert_reduce_fusion
  15.7 11.2 %all-reduce = (f32[4]{0:T(128)S(1)}, f32[4]{0:T(128)S(1)}) all-reduce(f32[4]{0:T(128)S(1)} %get-tuple-element.13, f32[4]{0:T(128)S(1)} %get-tuple-element.12), channel_id=1, replica_groups=mesh['pipe'=4,'dp'=4,'tensor'=2] {'dp'}, use_global_device_ids=true, to_apply=%region_8.9 | all-reduce | flops 8 | bytes 64 | tf_op jit(solution)/shard_map/psum | solution.py:77
  26.9 3.7 %fusion.52 = bf16[2,128,512]{2,1,0:T(8,128)(2,1)S(1)} fusion(bf16[2,1,512,2048]{3,2,1,0:T(8,128)(2,1)} %param.10, f32[2,2048]{1,0:T(2,128)S(1)} %bitcast.136, bf16[3,2,1,128,2048]{4,3,1,2,0:T(8,128)(2,1)S(1)} %bitcast.124), kind=kOutput, calls=%fused_computation.46 | convolution fusion | flops 538574848 | bytes 5521408 | tf_op jit(solution)/shard_map/vrd,vkd->vrk/dot_general | solution.py:28
  30.7 2.3 all-gather
  33.0 1.1 reduce_sum.120
  34.1 0.2 reduce_window_sum.14
  34.3 1.4 fusion.93
  35.7 4.9 %fusion.33 = bf16[2,128,2048]{2,1,0:T(8,128)(2,1)} fusion(bf16[2,1,512,2048]{3,2,1,0:T(8,128)(2,1)} %param.10, bf16[2,1,128,2048]{3,2,1,0:T(8,128)(2,1)} %param.13, f32[2,128]{1,0:T(2,128)S(1)} %fusion.121, f32[2,2048]{1,0:T(2,128)S(1)} %bitcast.137, bf16[3,2,1,128,2048]{4,3,1,2,0:T(8,128)(2,1)S(1)} %bitcast.125, f32[2,128]{1,0:T(2,128)S(1)} %get-tuple-element.22, ...), kind=kOutput, calls=%fused_computation.32 | convolution fusion | flops 542244864 | bytes 7882752 | tf_op jit(solution)/shard_map/vrk,vkd->vrd/dot_general | solution.py:41
  40.6 3.6 %collective-permute-start = (bf16[2,128,2048]{2,1,0:T(8,128)(2,1)}, bf16[2,128,2048]{2,1,0:T(8,128)(2,1)}, u32[]{:S(2)}, u32[]{:S(2)}) collective-permute-start(bf16[2,128,2048]{2,1,0:T(8,128)(2,1)} %fusion.33), channel_id=1, source_target_pairs={{0,24},{8,0},{16,8},{24,16},{1,25},{9,1},{17,9},{25,17},{2,26},{10... | collective-permute-start | bytes 3145736 | tf_op jit(solution)/shard_map/ppermute | solution.py:17
  44.3 0.2 select_reduce_fusion.1
  44.4 0.1 select_reduce_fusion
  44.5 1.6 multiply_convert_fusion
  46.2 21.0 %collective-permute-done = bf16[2,128,2048]{2,1,0:T(8,128)(2,1)} collective-permute-done((bf16[2,128,2048]{2,1,0:T(8,128)(2,1)}, bf16[2,128,2048]{2,1,0:T(8,128)(2,1)}, u32[]{:S(2)}, u32[]{:S(2)}) %collective-permute-start) | collective-permute-done | bytes 1048608 | tf_op jit(solution)/shard_map/ppermute | solution.py:17
  67.2 1.3 slice_select_fusion.3
  68.5 0.8 copy-done.11
  69.3 0.1 copy-done.13
  69.5 2.2 fusion.46
  71.8 3.7 %fusion.55 = bf16[2,128,512]{2,1,0:T(8,128)(2,1)S(1)} fusion(bf16[2,1,512,2048]{3,2,1,0:T(8,128)(2,1)} %param.10, f32[2,2048]{1,0:T(2,128)S(1)} %bitcast.138, bf16[3,2,1,128,2048]{4,3,1,2,0:T(8,128)(2,1)S(1)} %bitcast.126), kind=kOutput, calls=%fused_computation.47 | convolution fusion | flops 538574848 | bytes 5521408 | tf_op jit(solution)/shard_map/vrd,vkd->vrk/dot_general | solution.py:28
  75.5 2.3 all-gather.1
  77.8 1.2 reduce_sum.128
  79.0 12.1 %all-reduce.7.cloned.1.call-done = bf16[2,128,512]{2,1,0:T(8,128)(2,1)} async-done(((bf16[2,128,512]{2,1,0:T(8,128)(2,1)}), bf16[2,128,512]{2,1,0:T(8,128)(2,1)}) %all-reduce.7.cloned.1.call-update) | async-done | bytes 262160 | tf_op jit(solution)/shard_map/psum | solution.py:32
  91.1 1.4 fusion.101
  92.5 5.0 %fusion.39 = bf16[2,128,2048]{2,1,0:T(8,128)(2,1)} fusion(f32[2,128]{1,0:T(2,128)S(1)} %fusion.123, bf16[2,1,512,2048]{3,2,1,0:T(8,128)(2,1)} %param.10, f32[2,2048]{1,0:T(2,128)S(1)} %bitcast.139, bf16[3,2,1,128,2048]{4,3,1,2,0:T(8,128)(2,1)S(1)} %bitcast.127, bf16[1,128,2048]{2,1,0:T(8,128)(2,1)} %copy-done.13, bf16[1,128,2048]{2,1,0:T(8,128)(2,1)} %copy-done.11, ...), kind=kOutput, calls=%fused_computation.36 | convolution fusion | flops 542769152 | bytes 7882752 | tf_op jit(solution)/shard_map/vrk,vkd->vrd/dot_general | solution.py:41
  97.4 3.6 %collective-permute-start.1 = (bf16[2,128,2048]{2,1,0:T(8,128)(2,1)}, bf16[2,128,2048]{2,1,0:T(8,128)(2,1)}, u32[]{:S(2)}, u32[]{:S(2)}) collective-permute-start(bf16[2,128,2048]{2,1,0:T(8,128)(2,1)} %fusion.39), channel_id=1, source_target_pairs={{0,24},{8,0},{16,8},{24,16},{1,25},{9,1},{17,9},{25,17},{2,26},{10... | collective-permute-start | bytes 3145736 | tf_op jit(solution)/shard_map/ppermute | solution.py:17
  101.1 1.5 fusion.58
  102.6 2.5 all-gather.2
  105.1 1.1 reduce_sum.130
  106.3 6.0 %fusion.62 = f32[2,512,2048]{2,1,0:T(8,128)} fusion(bf16[2,1,128,2048]{3,2,1,0:T(8,128)(2,1)} %param.13, bf16[2,128,512]{2,1,0:T(8,128)(2,1)} %copy-done.5, f32[2,128]{1,0:T(2,128)S(1)} %get-tuple-element.22), kind=kOutput, calls=%fused_computation.55 | convolution fusion | flops 537788416 | bytes 9700352 | tf_op jit(solution)/shard_map/vrk,vrd->vkd/dot_general | solution.py:40
  112.3 4.6 %fusion.110 = f32[2,512,2048]{2,1,0:T(8,128)} fusion(bf16[1,128,2048]{2,1,0:T(8,128)(2,1)S(1)} %copy-done.14, bf16[1,128,2048]{2,1,0:T(8,128)(2,1)S(1)} %copy-done.12, bf16[2,128,512]{2,1,0:T(8,128)(2,1)S(1)} %copy-done.7, f32[2,128]{1,0:T(2,128)S(1)} %get-tuple-element.21), kind=kOutput, calls=%fused_computation.106 | convolution fusion | flops 538312704 | bytes 9700352 | tf_op jit(solution)/shard_map/vrk,vrd->vkd/dot_general | solution.py:40
  116.9 7.3 %collective-permute-done.1 = bf16[2,128,2048]{2,1,0:T(8,128)(2,1)} collective-permute-done((bf16[2,128,2048]{2,1,0:T(8,128)(2,1)}, bf16[2,128,2048]{2,1,0:T(8,128)(2,1)}, u32[]{:S(2)}, u32[]{:S(2)}) %collective-permute-start.1) | collective-permute-done | bytes 1048608 | tf_op jit(solution)/shard_map/ppermute | solution.py:17
  124.2 1.3 slice_select_fusion.1
  125.6 0.8 copy-done.9
  126.3 0.2 copy-done.10
  126.5 2.2 fusion.49
  128.8 9.5 %add_convert_fusion = bf16[2,512,2048]{2,1,0:T(8,128)(2,1)} fusion(f32[2,512,2048]{2,1,0:T(8,128)} %fusion.62, f32[2,512,2048]{2,1,0:T(8,128)} %fusion.110, bf16[1,128,2048]{2,1,0:T(8,128)(2,1)} %copy-done.10, bf16[1,128,2048]{2,1,0:T(8,128)(2,1)} %copy-done.9, bf16[2,128,512]{2,1,0:T(8,128)(2,1)S(1)} %reduce_sum.130, f32[2,128]{1,0:T(2,128)S(1)} %get-tuple-element.20), kind=kOutput, calls=%fused_computation | convolution fusion | flops 544604160 | bytes 22283264 | tf_op jit(solution)/shard_map/vrk,vrd->vkd/dot_general | solution.py:40
  138.4 5.7 %fusion.74 = f32[2,512,2048]{2,1,0:T(8,128)} fusion(f32[2,2048]{1,0:T(2,128)S(1)} %bitcast.141, bf16[3,2,1,128,2048]{4,3,1,2,0:T(8,128)(2,1)S(1)} %bitcast.129, f32[2,128]{1,0:T(2,128)S(1)} %get-tuple-element.22, bf16[2,128,512]{2,1,0:T(8,128)(2,1)} %copy-done.5, bf16[2,128,512]{2,1,0:T(8,128)(2,1)} %all-reduce.5.cloned.1.call-done), kind=kOutput, calls=%fused_computation.59 | convolution fusion | flops 540147712 | bytes 9978880 | tf_op jit(solution)/shard_map/vrk,vrd->vkd/dot_general | solution.py:39
  144.1 4.6 %fusion.71 = f32[2,512,2048]{2,1,0:T(8,128)} fusion(f32[2,2048]{1,0:T(2,128)S(1)} %bitcast.142, bf16[3,2,1,128,2048]{4,3,1,2,0:T(8,128)(2,1)S(1)} %bitcast.130, f32[2,128]{1,0:T(2,128)S(1)} %get-tuple-element.21, bf16[2,128,512]{2,1,0:T(8,128)(2,1)S(1)} %copy-done.8, bf16[2,128,512]{2,1,0:T(8,128)(2,1)S(1)} %copy-done.15), kind=kOutput, calls=%fused_computation.58 | convolution fusion | flops 540147712 | bytes 9978880 | tf_op jit(solution)/shard_map/vrk,vrd->vkd/dot_general | solution.py:39
  148.7 0.3 all-reduce.9.cloned.1.call-done
  149.0 9.4 %add_convert_fusion.1 = bf16[2,512,2048]{2,1,0:T(8,128)(2,1)} fusion(f32[2,512,2048]{2,1,0:T(8,128)} %fusion.74, f32[2,512,2048]{2,1,0:T(8,128)} %fusion.71, f32[2,2048]{1,0:T(2,128)S(1)} %bitcast.143, bf16[3,2,1,128,2048]{4,3,1,2,0:T(8,128)(2,1)S(1)} %bitcast.131, f32[2,128]{1,0:T(2,128)S(1)} %get-tuple-element.20, ...), kind=kOutput, calls=%fused_computation.1 | convolution fusion | flops 546439168 | bytes 22561792 | tf_op jit(solution)/shard_map/vrk,vrd->vkd/dot_general | solution.py:39
  158.4 1.4 fusion.109
  159.8 4.9 %fusion.61 = bf16[2,1,128,2048]{3,2,1,0:T(8,128)(2,1)} fusion(f32[2,128]{1,0:T(2,128)S(1)} %fusion.125, bf16[2,1,512,2048]{3,2,1,0:T(8,128)(2,1)} %param.10, f32[2,2048]{1,0:T(2,128)S(1)} %bitcast.144, bf16[3,2,1,128,2048]{4,3,1,2,0:T(8,128)(2,1)S(1)} %bitcast.132, bf16[1,128,2048]{2,1,0:T(8,128)(2,1)} %copy-done.10, bf16[1,128,2048]{2,1,0:T(8,128)(2,1)} %copy-done.9, ...), kind=kOutput, calls=%fused_computation.49 | convolution fusion | flops 542769152 | bytes 7882752 | tf_op jit(solution)/shard_map/vrk,vkd->vrd/dot_general | solution.py:41
  164.7 41.0 %reduce-scatter.5.cloned.1.call-done = bf16[2,128,2048]{2,1,0:T(8,128)(2,1)} async-done(((bf16[2,512,2048]{2,1,0:T(8,128)(2,1)}), bf16[2,128,2048]{2,1,0:T(8,128)(2,1)}) %reduce-scatter.5.cloned.1.call-update) | async-done | bytes 1048592 | tf_op jit(solution)/shard_map/reduce_scatter | solution.py:116
  205.7 2.8 %multiply_bitcast_fusion = f32[2,1,128,2048]{3,2,1,0:T(8,128)} fusion(bf16[2,128,2048]{2,1,0:T(8,128)(2,1)} %reduce-scatter.5.cloned.1.call-done), kind=kLoop, calls=%fused_computation.40 | loop fusion | flops 1048576 | bytes 3145728
  208.4 52.7 %reduce-scatter.3.cloned.1.call-done = bf16[2,128,2048]{2,1,0:T(8,128)(2,1)} async-done(((bf16[2,512,2048]{2,1,0:T(8,128)(2,1)}), bf16[2,128,2048]{2,1,0:T(8,128)(2,1)}) %reduce-scatter.3.cloned.1.call-update) | async-done | bytes 1048592 | tf_op jit(solution)/shard_map/reduce_scatter | solution.py:113
  261.1 2.8 %multiply_bitcast_fusion.1 = f32[2,1,128,2048]{3,2,1,0:T(8,128)} fusion(bf16[2,128,2048]{2,1,0:T(8,128)(2,1)} %reduce-scatter.3.cloned.1.call-done), kind=kLoop, calls=%fused_computation.41 | loop fusion | flops 1048576 | bytes 3145728
  (59 shorter events, 0.5 us)
Async XLA Ops:
  7.2 5.1 %copy-start.16 = (f32[2,1,2048]{2,1,0:T(1,128)S(1)}, f32[2,1,2048]{2,1,0:T(1,128)}, u32[]{:S(2)}) copy-start(f32[2,1,2048]{2,1,0:T(1,128)} %param.12) | copy-start | bytes 49156
  7.2 5.1 %copy-start = (bf16[3,2,1,128,2048]{4,3,2,1,0:T(8,128)(2,1)S(1)}, bf16[3,2,1,128,2048]{4,3,2,1,0:T(8,128)(2,1)}, u32[]{:S(2)}) copy-start(bf16[3,2,1,128,2048]{4,3,2,1,0:T(8,128)(2,1)} %param.9) | copy-start | bytes 9437188
  7.2 8.4 %copy-start.18 = (s32[2,1,4]{2,1,0:T(1,128)S(1)}, s32[2,1,4]{2,1,0:T(1,128)}, u32[]{:S(2)}) copy-start(s32[2,1,4]{2,1,0:T(1,128)} %param.17) | copy-start | bytes 100
  7.2 8.4 %copy-start.17 = (f32[2,1,4]{2,1,0:T(1,128)S(1)}, f32[2,1,4]{2,1,0:T(1,128)}, u32[]{:S(2)}) copy-start(f32[2,1,4]{2,1,0:T(1,128)} %param.15) | copy-start | bytes 100
  7.2 27.1 %all-reduce.5.cloned.1.call-start = ((), (), s32[]{:S(2)}) async-start(), calls=%async_computation.2 | async-start | bytes 524288 | tf_op jit(solution)/shard_map/psum | solution.py:32
  12.2 78.9 %all-reduce.7.cloned.1.call-start = ((), (), s32[]{:S(2)}) async-start(), calls=%async_computation.3 | async-start | bytes 524288 | tf_op jit(solution)/shard_map/psum | solution.py:32
  26.9 7.2 %copy-start.19 = (s32[2,1,4]{2,1,0:T(1,128)S(1)}, s32[2,1,4]{2,1,0:T(1,128)}, u32[]{:S(2)}) copy-start(s32[2,1,4]{2,1,0:T(1,128)} %param.16) | copy-start | bytes 100
  34.1 6.5 %copy-start.5 = (bf16[2,128,512]{2,1,0:T(8,128)(2,1)}, bf16[2,128,512]{2,1,0:T(8,128)(2,1)S(1)}, u32[]{:S(2)}) copy-start(bf16[2,128,512]{2,1,0:T(8,128)(2,1)S(1)} %reduce_sum.120) | copy-start | bytes 786436
  40.6 26.6 %collective-permute-start = (bf16[2,128,2048]{2,1,0:T(8,128)(2,1)}, bf16[2,128,2048]{2,1,0:T(8,128)(2,1)}, u32[]{:S(2)}, u32[]{:S(2)}) collective-permute-start(bf16[2,128,2048]{2,1,0:T(8,128)(2,1)} %fusion.33), channel_id=1, source_target_pairs={{0,24},{8,0},{16,8},{24,16},{1,25},{9,1},{17,9},{25,17},{2,26},{10... | collective-permute-start | bytes 3145736 | tf_op jit(solution)/shard_map/ppermute | solution.py:17
  44.5 24.9 %copy-start.1 = (bf16[2,1,512,2048]{3,2,1,0:T(8,128)(2,1)S(1)}, bf16[2,1,512,2048]{3,2,1,0:T(8,128)(2,1)}, u32[]{:S(2)}) copy-start(bf16[2,1,512,2048]{3,2,1,0:T(8,128)(2,1)} %param.11) | copy-start | bytes 12582916
  46.1 21.1 %copy-start.3 = (bf16[2,128,2048]{2,1,0:T(8,128)(2,1)}, bf16[2,128,2048]{2,1,0:T(8,128)(2,1)S(1)}, u32[]{:S(2)}) copy-start(bf16[2,128,2048]{2,1,0:T(8,128)(2,1)S(1)} %multiply_convert_fusion) | copy-start | bytes 3145732
  68.5 0.8 copy-start.11
  68.5 1.0 copy-start.13
  71.7 77.3 %all-reduce.9.cloned.1.call-start = ((), (), s32[]{:S(2)}) async-start(), calls=%async_computation.4 | async-start | bytes 524288 | tf_op jit(solution)/shard_map/psum | solution.py:32
  79.0 18.5 %copy-start.6 = (bf16[2,128,512]{2,1,0:T(8,128)(2,1)}, bf16[2,128,512]{2,1,0:T(8,128)(2,1)S(1)}, u32[]{:S(2)}) copy-start(bf16[2,128,512]{2,1,0:T(8,128)(2,1)S(1)} %reduce_sum.128) | copy-start | bytes 786436
  92.4 8.6 %copy-start.20 = (bf16[2,1,512,2048]{3,2,1,0:T(8,128)(2,1)S(1)}, bf16[2,1,512,2048]{3,2,1,0:T(8,128)(2,1)}, u32[]{:S(2)}) copy-start(bf16[2,1,512,2048]{3,2,1,0:T(8,128)(2,1)} %param.10) | copy-start | bytes 12582916
  97.4 26.8 %collective-permute-start.1 = (bf16[2,128,2048]{2,1,0:T(8,128)(2,1)}, bf16[2,128,2048]{2,1,0:T(8,128)(2,1)}, u32[]{:S(2)}, u32[]{:S(2)}) collective-permute-start(bf16[2,128,2048]{2,1,0:T(8,128)(2,1)} %fusion.39), channel_id=1, source_target_pairs={{0,24},{8,0},{16,8},{24,16},{1,25},{9,1},{17,9},{25,17},{2,26},{10... | collective-permute-start | bytes 3145736 | tf_op jit(solution)/shard_map/ppermute | solution.py:17
  106.2 6.0 %copy-start.7 = (bf16[2,128,512]{2,1,0:T(8,128)(2,1)S(1)}, bf16[2,128,512]{2,1,0:T(8,128)(2,1)}, u32[]{:S(2)}) copy-start(bf16[2,128,512]{2,1,0:T(8,128)(2,1)} %copy-done.6) | copy-start | bytes 786436
  106.2 6.0 %copy-start.12 = (bf16[1,128,2048]{2,1,0:T(8,128)(2,1)S(1)}, bf16[1,128,2048]{2,1,0:T(8,128)(2,1)}, u32[]{:S(2)}) copy-start(bf16[1,128,2048]{2,1,0:T(8,128)(2,1)} %copy-done.11) | copy-start | bytes 1572868
  106.3 6.0 %copy-start.14 = (bf16[1,128,2048]{2,1,0:T(8,128)(2,1)S(1)}, bf16[1,128,2048]{2,1,0:T(8,128)(2,1)}, u32[]{:S(2)}) copy-start(bf16[1,128,2048]{2,1,0:T(8,128)(2,1)} %copy-done.13) | copy-start | bytes 1572868
  112.3 11.9 %copy-start.4 = (bf16[2,128,2048]{2,1,0:T(8,128)(2,1)S(1)}, bf16[2,128,2048]{2,1,0:T(8,128)(2,1)}, u32[]{:S(2)}) copy-start(bf16[2,128,2048]{2,1,0:T(8,128)(2,1)} %copy-done.3) | copy-start | bytes 3145732
  112.3 14.2 %copy-start.2 = (bf16[2,1,512,2048]{3,2,1,0:T(8,128)(2,1)S(1)}, bf16[2,1,512,2048]{3,2,1,0:T(8,128)(2,1)}, u32[]{:S(2)}) copy-start(bf16[2,1,512,2048]{3,2,1,0:T(8,128)(2,1)} %param.11) | copy-start | bytes 12582916
  125.5 0.8 copy-start.9
  125.6 1.0 copy-start.10
  128.8 76.9 %reduce-scatter.5.cloned.1.call-start = ((), (), s32[]{:S(2)}) async-start(), calls=%async_computation.6 | async-start | bytes 5242880 | tf_op jit(solution)/shard_map/reduce_scatter | solution.py:116
  138.3 122.8 %reduce-scatter.3.cloned.1.call-start = ((), (), s32[]{:S(2)}) async-start(), calls=%async_computation.5 | async-start | bytes 5242880 | tf_op jit(solution)/shard_map/reduce_scatter | solution.py:113
  138.3 5.8 %copy-start.8 = (bf16[2,128,512]{2,1,0:T(8,128)(2,1)S(1)}, bf16[2,128,512]{2,1,0:T(8,128)(2,1)}, u32[]{:S(2)}) copy-start(bf16[2,128,512]{2,1,0:T(8,128)(2,1)} %copy-done.6) | copy-start | bytes 786436
  138.3 5.7 %copy-start.15 = (bf16[2,128,512]{2,1,0:T(8,128)(2,1)S(1)}, bf16[2,128,512]{2,1,0:T(8,128)(2,1)}, u32[]{:S(2)}) copy-start(bf16[2,128,512]{2,1,0:T(8,128)(2,1)} %all-reduce.7.cloned.1.call-done) | copy-start | bytes 786436
Sparse Core Ops, SparseCore 0:
  12.3 20.9 all-reduce.4
  71.8 19.1 all-reduce.6
  128.9 20.0 all-reduce.8
  151.8 53.7 reduce-scatter.4
  208.5 52.5 reduce-scatter.2
